TPU v7x, 32 devices: a whole 2x2x4 slice. The times are simulated.
32 devices in a mesh: row: 4 (over z), col: 8 (over y, x, core).
Axes of the slice: x: 2, y: 2, z: 4, core: 2. Of those that a mesh axis runs over, the one named last changes fastest.
Arguments:
- tokens: bfloat16 [4096, 4096], P(('row', 'col')), may hold values from -6 to 6
- router_logits: float32 [4096, 32], P(('row', 'col')), may hold values from -15 to 320
- expert_ids: int32 [4096, 8], P(('row', 'col')), may hold values from 0 to 31, all different within a row; in each aligned block of 128 rows (0 to 127, 128 to 255, ...) at most 48 rows name the same one
- w_gate: bfloat16 [32, 4096, 768], P(('row', 'col')), may hold values from -0.09375 to 0.09375
- w_up: bfloat16 [32, 4096, 768], P(('row', 'col')), may hold values from -0.09375 to 0.09375
- w_down: bfloat16 [32, 768, 4096], P(('row', 'col')), may hold values from -0.21875 to 0.21875
Outputs:
- mixed: bfloat16 [4096, 4096], P(('row', 'col'))
- balance_loss: float32 [], replicated
Inputs may be any that keep to these rules, and one draw needn't show every extreme that they name: `expert_ids`: each row names 8 different experts. In the 128 rows of one device no expert is named by more than 48 rows, a bound that some block reaches.
All inputs are finite; a program needn't handle non-finite values.
Results may differ from a plain program's by a relative error of at most 0.0015.
The roundings to bfloat16 on the way count: a program that leaves them out, or rounds other values in their place, can miss the bound.
Values may be sent and summed in bfloat16 or wider, within the bound.
A program may use at most 128 MiB of HBM per device.

v0:
```python
import jax
import jax.numpy as jnp
from jax import lax
from jax.sharding import PartitionSpec as P


def slot_table(expert_ids, experts, capacity):
    flattened = expert_ids.reshape(-1)
    onehot = (flattened[:, None] == jnp.arange(experts, dtype=jnp.int32)[None, :]).astype(jnp.int32)
    earlier = jnp.cumsum(onehot, axis=0) - onehot
    slot_of = jnp.sum(earlier * onehot, axis=1)
    position = flattened * capacity + slot_of
    return (onehot, position)


def expert_ffn(slot_rows, w_gate, w_up, w_down):
    shaped = slot_rows.reshape(-1, slot_rows.shape[-1])
    gate_act = jnp.dot(shaped, w_gate[0], preferred_element_type=jnp.float32)
    up_act = jnp.dot(shaped, w_up[0], preferred_element_type=jnp.float32)
    hidden = (jax.nn.silu(gate_act) * up_act).astype(jnp.bfloat16)
    result = jnp.dot(hidden, w_down[0], preferred_element_type=jnp.float32).astype(jnp.bfloat16)
    return result.reshape(slot_rows.shape)


def local(tokens, router_logits, expert_ids, w_gate, w_up, w_down):
    tok_rows, top_k = expert_ids.shape
    width = tokens.shape[1]
    experts = router_logits.shape[1]
    n_row = lax.axis_size("row")
    n_col = lax.axis_size("col")
    capacity = 3 * tok_rows * top_k // (2 * experts)
    onehot, position = slot_table(expert_ids, experts, capacity)
    probs = jax.nn.softmax(router_logits, axis=1)
    counts = jnp.sum(onehot, axis=0).astype(jnp.float32)
    prob_sum = jnp.sum(probs, axis=0)
    total_counts, total_probs = lax.psum((counts, prob_sum), ("row", "col"))
    chosen = jnp.take_along_axis(probs, expert_ids, axis=1)
    weights = chosen / jnp.sum(chosen, axis=1, keepdims=True)
    source = jnp.arange(tok_rows * top_k, dtype=jnp.int32) // top_k
    owner = jnp.full((experts * capacity,), -1, jnp.int32).at[position].set(source)
    present = owner >= 0
    picked = tokens[jnp.maximum(owner, 0)]
    send_rows = jnp.where(present[:, None], picked, jnp.zeros((), jnp.bfloat16)).reshape(
        experts, capacity, width
    )
    outputs = expert_ffn(
        lax.all_to_all(send_rows, ("row", "col"), split_axis=0, concat_axis=0, tiled=True),
        w_gate,
        w_up,
        w_down,
    )
    returned = lax.all_to_all(outputs, ("row", "col"), split_axis=0, concat_axis=0, tiled=True)
    gathered = returned.reshape(experts * capacity, width)[position].reshape(tok_rows, top_k, width)
    mixed = jnp.zeros((tok_rows, width), jnp.float32)
    for slot_k in range(top_k):
        mixed = mixed + weights[:, slot_k : slot_k + 1] * gathered[:, slot_k].astype(jnp.float32)
    tokens_all = tok_rows * n_row * n_col
    balance_loss = experts * jnp.sum(
        total_counts / (tokens_all * top_k) * (total_probs / tokens_all)
    )
    return (mixed.astype(jnp.bfloat16), balance_loss)


def solution(mesh):
    placed = (
        P(("row", "col"), None),
        P(("row", "col"), None),
        P(("row", "col"), None),
        P(("row", "col"), None, None),
        P(("row", "col"), None, None),
        P(("row", "col"), None, None),
    )
    return jax.shard_map(
        local, mesh=mesh, in_specs=placed, out_specs=(P(("row", "col"), None), P()), check_vma=False
    )
```

profile of v0, /device:TPU:0, one launch (start us, length us, event | category | flops | bytes accessed | tf_op | source)
XLA Modules:
  0.0 746.6 jit_solution(10778036567166298374)
XLA Ops:
  0.6 0.0 copy-start
  0.6 0.9 copy.55
  1.5 0.1 eq.29
  1.6 0.1 eq.25
  1.7 0.7 broadcast_multiply_fusion
  2.4 9.0 %reduce-window.6 = s32[32,8,128]{2,1,0:T(8,128)S(1)} reduce-window(s32[32,8,128]{2,1,0:T(8,128)S(1)} %fusion.17, s32[]{:T(128)} %constant.30.clone.1), window={size=1x1x128 pad=0_0x0_0x127_0}, to_apply=%region_3.4 | reduce-window | flops 4161536 | bytes 262148 | tf_op jit(solution)/shard_map/reduce-window
  11.4 0.1 slice.78
  11.5 0.1 copy.57
  11.7 0.1 copy.58
  11.8 0.1 broadcast_add_fusion
  11.9 0.1 copy.54
  12.0 0.1 mul.113
  12.1 0.1 convert_reduce_fusion
  12.2 4.3 scatter_custom_fusion
  16.6 0.1 broadcast_in_dim.33
  16.7 0.0 copy-done
  16.7 9.5 %gather_fusion = bf16[1536,4096]{1,0:T(8,128)(2,1)} fusion(bf16[128,4096]{1,0:T(8,128)(2,1)S(1)} %copy-done, s32[2048]{0:T(1024)S(1)} %pad_clamp_fusion), kind=kCustom, calls=%fused_computation | custom fusion | bytes 25171968 | tf_op jit(solution)/shard_map/gather | solution.py:42
  26.2 6.4 broadcast_select_fusion
  32.6 0.0 copy-start.4
  32.6 280.5 %all_to_all.10 = bf16[32,48,4096]{2,1,0:T(8,128)(2,1)S(1)} all-to-all(bf16[32,48,4096]{2,1,0:T(8,128)(2,1)S(1)} %broadcast_select_fusion), channel_id=1, replica_groups=mesh['row'=4,'col'=8] {'row','col'}, dimensions={0} | all-to-all | bytes 25165824 | tf_op jit(solution)/shard_map/all_to_all | solution.py:47
  313.1 0.0 copy-done.4
  313.1 0.0 slice-start
  313.1 11.4 %fusion.1 = f32[1536,768]{1,0:T(8,128)} fusion(bf16[1536,4096]{1,0:T(8,128)(2,1)S(1)} %bitcast.94, bf16[1,4096,768]{2,1,0:T(8,128)(2,1)S(1)} %copy-done.4), kind=kOutput, calls=%fused_computation.7 | convolution fusion | flops 9663676416 | bytes 23592960 | tf_op jit(solution)/shard_map/dot_general | solution.py:19
  324.6 0.0 slice-start.1
  324.6 14.4 %multiply_convert_fusion = bf16[1536,768]{1,0:T(8,128)(2,1)} fusion(f32[1536,768]{1,0:T(8,128)} %fusion.1, bf16[1536,4096]{1,0:T(8,128)(2,1)S(1)} %bitcast.95, bf16[1,4096,768]{2,1,0:T(8,128)(2,1)} %param.9), kind=kOutput, calls=%fused_computation.11 | convolution fusion | flops 9670754304 | bytes 25952256 | tf_op jit(solution)/shard_map/dot_general | solution.py:18
  339.0 0.0 slice-done
  339.0 0.0 slice-done.1
  339.0 13.9 %convolution_convert_fusion = bf16[1536,4096]{1,0:T(8,128)(2,1)} fusion(bf16[1536,768]{1,0:T(8,128)(2,1)} %multiply_convert_fusion, bf16[1,768,4096]{2,1,0:T(8,128)(2,1)S(1)} %bitcast.102), kind=kOutput, calls=%fused_computation.4 | convolution fusion | flops 9669967872 | bytes 21233664 | tf_op jit(solution)/shard_map/dot_general | solution.py:21
  352.9 0.0 copy-start.2
  352.9 0.0 copy-start.3
  352.9 3.9 all-to-all-start.1
  356.8 0.0 copy-done.2
  356.9 0.1 fusion.26
  357.0 297.6 %all-reduce = (f32[32]{0:T(128)S(1)}, f32[32]{0:T(128)S(1)}) all-reduce(f32[32]{0:T(128)S(1)} %get-tuple-element.6, f32[32]{0:T(128)S(1)} %convert_element_type.88), channel_id=1, replica_groups=mesh['row'=4,'col'=8] {'row','col'}, use_global_device_ids=true, to_apply=%region_10.11 | all-reduce | flops 64 | bytes 512 | tf_op jit(solution)/shard_map/psum | solution.py:36
  654.5 0.0 copy-done.3
  654.6 0.1 copy.52
  654.7 0.1 reshape.128
  654.8 7.0 gather_fusion.2
  661.8 0.1 reshape.131
  661.9 0.6 multiply_reduce_fusion
  663.3 0.0 all-to-all-done.1
  663.3 21.3 %gather_fusion.1 = bf16[1024,4096]{1,0:T(8,128)(2,1)} fusion(bf16[1536,4096]{1,0:T(8,128)(2,1)} %bitcast.12, s32[1024]{0:T(1024)S(1)} %broadcast_clamp_fusion), kind=kCustom, calls=%fused_computation.1 | custom fusion | bytes 16781312 | tf_op jit(solution)/shard_map/gather | solution.py:53
  684.5 40.3 %fusion.28 = (bf16[128,1,4096]{2,1,0:T(2,128)(2,1)S(1)}, bf16[128,1,4096]{2,1,0:T(2,128)(2,1)S(1)}, bf16[128,1,4096]{2,1,0:T(2,128)(2,1)S(1)}, bf16[128,1,4096]{...) fusion(bf16[128,8,4096]{2,1,0:T(8,128)(2,1)} %bitcast.91), kind=kLoop, calls=%fused_computation.78 | loop fusion | bytes 16777216 | tf_op jit(solution)/shard_map/slice | solution.py:56
  724.8 0.0 copy-start.1
  724.8 20.7 %fusion.8 = bf16[128,4096]{1,0:T(8,128)(2,1)} fusion(bf16[128,1,4096]{2,1,0:T(2,128)(2,1)} %get-tuple-element.15, bf16[128,1,4096]{2,1,0:T(2,128)(2,1)S(1)} %get-tuple-element.9, bf16[128,1,4096]{2,1,0:T(2,128)(2,1)S(1)} %get-tuple-element.10, bf16[128,1,4096]{2,1,0:T(2,128)(2,1)S(1)} %get-tuple-element.11, bf16[128,1,4096]{2,1,0:T(2,128)(2,1)} %get-tuple-element.12, ...), kind=kLoop, calls=%fused_computation.14 | loop fusion | flops 12582912 | bytes 9441280 | tf_op jit(solution)/shard_map/convert_element_type | solution.py:61
  745.5 0.0 copy-done.1
  (18 shorter events, 0.2 us)
Async XLA Ops:
  0.6 16.1 %copy-start = (bf16[128,4096]{1,0:T(8,128)(2,1)S(1)}, bf16[128,4096]{1,0:T(8,128)(2,1)}, u32[]{:S(2)}) copy-start(bf16[128,4096]{1,0:T(8,128)(2,1)} %param.6) | copy-start | bytes 3145732
  32.6 280.5 %copy-start.4 = (bf16[1,4096,768]{2,1,0:T(8,128)(2,1)S(1)}, bf16[1,4096,768]{2,1,0:T(8,128)(2,1)}, u32[]{:S(2)}) copy-start(bf16[1,4096,768]{2,1,0:T(8,128)(2,1)} %param.10) | copy-start | bytes 18874372
  313.1 25.9 %slice-start = ((s8[6291456]{0:T(1024)(128)(4,1)}), s8[2097152]{0:T(1024)(128)(4,1)S(1)}, s32[]{:S(2)}) async-start(s8[6291456]{0:T(1024)(128)(4,1)} %bitcast.101), calls=%async_computation.2 | async-start | bytes 4194304
  324.6 14.4 %slice-start.1 = ((s8[6291456]{0:T(1024)(128)(4,1)}), s8[4194304]{0:T(1024)(128)(4,1)S(1)}, s32[]{:S(2)}) async-start(s8[6291456]{0:T(1024)(128)(4,1)} %bitcast.101), calls=%async_computation.3 | async-start | bytes 8388608
  352.9 3.9 copy-start.2
  352.9 301.7 %copy-start.3 = (s32[128,8]{0,1:T(8,128)S(1)}, s32[128,8]{0,1:T(8,128)}, u32[]{:S(2)}) copy-start(s32[128,8]{0,1:T(8,128)} %param.8) | copy-start | bytes 12292
  352.9 310.4 %all-to-all-start.1 = ((bf16[32,48,4096]{2,1,0:T(8,128)(2,1)}), bf16[32,48,4096]{2,1,0:T(8,128)(2,1)}, u32[]{:S(2)}, u32[]{:S(2)}) async-start(bf16[32,48,4096]{2,1,0:T(8,128)(2,1)} %bitcast.93), calls=%async_computation.1 | async-start | bytes 25165824 | tf_op jit(solution)/shard_map/all_to_all | solution.py:52
  724.8 20.7 %copy-start.1 = (bf16[128,4096]{1,0:T(8,128)(2,1)S(1)}, bf16[128,4096]{1,0:T(8,128)(2,1)}, u32[]{:S(2)}) copy-start(bf16[128,4096]{1,0:T(8,128)(2,1)} %param.6) | copy-start | bytes 3145732
where the time goes:
time: 747 us
  blocking collectives  578 us (77%)
  local copies, waits for them, and re-layouts  84.4 us (11%)
  matrix products  39.7 us (5%)
  other arithmetic  37.9 us (5%)
    psum x1, blocking collectives, local(): total_counts, total_probs = lax.psum((counts, prob_sum), ('row', 'col'))  298 us
    all_to_all x1, blocking collectives, local(): lax.all_to_all(send_rows, ('row', 'col'), split_axis=0, concat_axis=0, ti...  281 us
    slice x1, local copies, waits for them, and re-layouts, local(): gathered[:, slot_k].astype(jnp.float32)  40.3 us
    gather x1, local copies, waits for them, and re-layouts, local(): returned.reshape(experts * capacity, width)[position]  21.3 us
    convert_element_type x1, other arithmetic, local(): return (mixed.astype(jnp.bfloat16), balance_loss)  20.7 us
  transfers between devices with their start and end apart: 1, of which 0 were waited for; matrix products, arithmetic and copies ran while one was open for 1% of the time, Pallas kernels for 0%

commit v1 on v0

v1 whole, which is shorter than its diff:
```python
import jax
import jax.numpy as jnp
from jax import lax
from jax.sharding import PartitionSpec as P

BF16 = jnp.bfloat16
F32 = jnp.float32
AXES = ("row", "col")
CHUNKS = 4
GATHER_LIMIT = 64 * 1024 * 1024


def slots_before(hit):
    tok = hit.shape[-1]
    order = jnp.arange(tok, dtype=jnp.int32)
    upper = (order[:, None] < order[None, :]).astype(BF16)
    return jnp.dot(hit.astype(BF16), upper, preferred_element_type=F32)


def exchange_routes(router_logits, expert_ids):
    tok, top_k = expert_ids.shape
    experts = router_logits.shape[1]
    probs = jax.nn.softmax(router_logits, axis=1)
    names = jnp.arange(experts, dtype=jnp.int32)
    match = expert_ids[:, :, None] == names[None, None, :]
    chosen = jnp.sum(jnp.where(match, probs[:, None, :], 0.0), axis=2)
    weights = chosen / jnp.sum(chosen, axis=1, keepdims=True)
    prob_rows = -(-experts // tok)
    prob_sum = jnp.pad(jnp.sum(probs, axis=0), (0, prob_rows * tok - experts)).reshape(prob_rows, tok)
    packed = jnp.concatenate([expert_ids.astype(F32).T, weights.T, prob_sum], axis=0)
    routes = lax.all_gather(packed, AXES, axis=0, tiled=False)
    ids = routes[:, :top_k].astype(jnp.int32)
    mix = routes[:, top_k : 2 * top_k]
    prob_total = jnp.sum(routes[:, 2 * top_k :], axis=0).reshape(-1)[:experts]
    return ids, mix, prob_total


def local(tokens, router_logits, expert_ids, w_gate, w_up, w_down):
    tok, top_k = expert_ids.shape
    width = tokens.shape[1]
    experts = router_logits.shape[1]
    n_row = lax.axis_size("row")
    n_col = lax.axis_size("col")
    n_dev = n_row * n_col
    capacity = 3 * tok * top_k // (2 * experts)
    row, col = lax.axis_index("row"), lax.axis_index("col")
    me = row * n_col + col

    ids, mix, prob_total = exchange_routes(router_logits, expert_ids)
    names = jnp.arange(experts, dtype=jnp.int32)
    counts = jnp.sum((ids[..., None] == names).astype(F32), axis=(0, 1, 2))
    tokens_all = tok * n_dev
    balance_loss = experts * jnp.sum(counts / (tokens_all * top_k) * (prob_total / tokens_all))
    places = jnp.arange(capacity, dtype=F32)

    if tokens.size * tokens.dtype.itemsize * n_dev <= GATHER_LIMIT:
        hit = jnp.any(ids == me, axis=1)
        slot = slots_before(hit)
        pick = (hit[:, None, :] & (slot[:, None, :] == places[None, :, None])).astype(BF16)
        everyone = lax.all_gather(tokens, AXES, axis=0, tiled=False)
        rows = lax.dot_general(
            pick, everyone, (((2,), (1,)), ((0,), (0,))), preferred_element_type=F32
        ).astype(BF16)
    else:
        mine = lax.dynamic_index_in_dim(ids, me, 0, keepdims=False)
        hit = jnp.any(mine[None] == names[:, None, None], axis=1)
        slot = slots_before(hit)
        pick = (hit[:, None, :] & (slot[:, None, :] == places[None, :, None])).astype(BF16)
        picked = lax.dot_general(
            pick.reshape(-1, tok), tokens, (((1,), (0,)), ((), ())), preferred_element_type=F32
        ).astype(BF16)
        rows = lax.all_to_all(
            picked.reshape(experts, capacity, width), AXES, split_axis=0, concat_axis=0, tiled=True
        )
    shaped = rows.reshape(n_dev * capacity, width)
    gate_act = jnp.dot(shaped, w_gate[0], preferred_element_type=F32)
    up_act = jnp.dot(shaped, w_up[0], preferred_element_type=F32)
    hidden = (jax.nn.silu(gate_act) * up_act).astype(BF16)
    hidden = hidden.reshape(n_row, n_col, capacity, -1).swapaxes(0, 1).reshape(n_dev * capacity, -1)

    column_ids = lax.dynamic_index_in_dim(ids.reshape(n_row, n_col, top_k, tok), col, 1, keepdims=False)
    column_mix = lax.dynamic_index_in_dim(mix.reshape(n_row, n_col, top_k, tok), col, 1, keepdims=False)
    row_names = row * n_col + jnp.arange(n_col, dtype=jnp.int32)
    match = column_ids[:, None] == row_names[None, :, None, None]
    hit = jnp.any(match, axis=2)
    share = jnp.sum(jnp.where(match, column_mix[:, None], 0.0), axis=2)
    slot = slots_before(hit)
    here = slot[:, :, None, :] == places[None, None, :, None]
    high = lax.reduce_precision(share, 8, 7)
    low = lax.reduce_precision(share - high, 8, 7)

    def table(part):
        return jnp.where(here, part[:, :, None, :], 0.0).astype(BF16).reshape(n_row, n_col * capacity, tok)

    high, low = table(high), table(low)

    step = width // CHUNKS
    parts = []
    for chunk in range(CHUNKS):
        down = w_down[0][:, chunk * step : (chunk + 1) * step]
        result = jnp.dot(hidden, down, preferred_element_type=F32).astype(BF16)
        back = lax.all_to_all(
            result.reshape(n_col, n_row, capacity, step), "col", split_axis=0, concat_axis=0, tiled=True
        )
        back = back.swapaxes(0, 1).reshape(n_row, n_col * capacity, step)
        dims = (((1,), (1,)), ((0,), (0,)))
        partial = lax.dot_general(high, back, dims, preferred_element_type=F32)
        partial = partial + lax.dot_general(low, back, dims, preferred_element_type=F32)
        total = lax.psum_scatter(partial, "row", scatter_dimension=0, tiled=True)
        parts.append(total.reshape(tok, step).astype(BF16))
    return jnp.concatenate(parts, axis=1), balance_loss


def solution(mesh):
    placed = (
        P(AXES, None),
        P(AXES, None),
        P(AXES, None),
        P(AXES, None, None),
        P(AXES, None, None),
        P(AXES, None, None),
    )
    return jax.shard_map(
        local, mesh=mesh, in_specs=placed, out_specs=(P(AXES, None), P()), check_vma=False
    )
```

time: 747 us -> 498 us (0.67)
  blocking collectives: 578 us -> 167 us
  waiting for transfers between devices: 0.01 us -> 222 us
  local copies, waits for them, and re-layouts: 84.4 us -> 4.23 us
  matrix products: 39.7 us -> 71.4 us
  other arithmetic: 37.9 us -> 12.9 us
  between operations: 2.61 us -> 15.8 us
    psum x1 -> x0, blocking collectives: 298 us -> none  [local(): total_counts, total_probs = lax.psum((counts, prob_sum), ('row', 'col'))]
    all_to_all x1 -> x3, blocking collectives: 281 us -> 121 us  [local(): lax.all_to_all(result.reshape(n_col, n_row, capacity, step), 'col', split...]
    all_gather x0 -> x1, waiting for transfers between devices: none -> 150 us  [local(): everyone = lax.all_gather(tokens, AXES, axis=0, tiled=False)]
    all_gather x0 -> x1, blocking collectives: none -> 46.2 us  [exchange_routes(): routes = lax.all_gather(packed, AXES, axis=0, tiled=False)]
    slice x3 -> x0, local copies, waits for them, and re-layouts: 40.5 us -> none  [the longest x1 40.3 us: local(): gathered[:, slot_k].astype(jnp.float32)]
    gather x7 -> x0, local copies, waits for them, and re-layouts: 38.2 us -> none  [the longest x1 21.3 us: local(): returned.reshape(experts * capacity, width)[position]]
    all_to_all x1, waiting for transfers between devices: 0.01 us -> 35.8 us  [local(): lax.all_to_all(result.reshape(n_col, n_row, capacity, step), 'col', split...]
    reduce_scatter x0 -> x4, waiting for transfers between devices: none -> 34.6 us  [local(): total = lax.psum_scatter(partial, 'row', scatter_dimension=0, tiled=True)]
  transfers between devices with their start and end apart: 1 -> 6, of which waited for: 0 -> 3; matrix products, arithmetic and copies ran while one was open for 1% -> 7% of each run, Pallas kernels for 0% -> 0%
where the time goes in v1:
time: 498 us; the launch traced here: 497 us
  waiting for transfers between devices  222 us (45%)
  blocking collectives  167 us (34%)
  matrix products  71.4 us (14%)
  between operations  15.8 us (3%)
  other arithmetic  12.9 us (3%)
    all_gather x1, waiting for transfers between devices, local(): everyone = lax.all_gather(tokens, AXES, axis=0, tiled=False)  150 us
    all_to_all x3, blocking collectives, local(): lax.all_to_all(result.reshape(n_col, n_row, capacity, step), 'col', split...  121 us
    all_gather x1, blocking collectives, exchange_routes(): routes = lax.all_gather(packed, AXES, axis=0, tiled=False)  46.2 us
    all_to_all x1, waiting for transfers between devices, local(): lax.all_to_all(result.reshape(n_col, n_row, capacity, step), 'col', split...  35.8 us
    reduce_scatter x4, waiting for transfers between devices, local(): total = lax.psum_scatter(partial, 'row', scatter_dimension=0, tiled=True)  34.6 us
    dot_general x4, matrix products, local(): result = jnp.dot(hidden, down, preferred_element_type=F32).astype(BF16)  18.9 us
    dot_general x1, matrix products, local(): up_act = jnp.dot(shaped, w_up[0], preferred_element_type=F32)  15.3 us
    dot_general x1, matrix products, local(): gate_act = jnp.dot(shaped, w_gate[0], preferred_element_type=F32)  13 us
  transfers between devices with their start and end apart: 6, of which 3 were waited for; matrix products, arithmetic and copies ran while one was open for 7% of the time, Pallas kernels for 0%

profile of v1, /device:TPU:0, one launch (start us, length us, event | category | flops | bytes accessed | tf_op | source)
XLA Modules:
  0.0 497.0 jit_solution(16408911850105412138)
XLA Ops:
  7.2 0.7 all-gather.5.cloned.1.call-update
  7.9 0.7 reduce_max.9
  8.6 0.7 fusion.22
  9.4 0.8 fusion.24
  10.2 0.7 select_reduce_fusion
  11.0 0.7 convert_bitcast_fusion.4
  11.7 46.2 %all-gather.2 = f32[32,17,128]{2,1,0:T(8,128)S(1)} all-gather(f32[1,17,128]{2,1,0:T(8,128)S(1)} %maximum_bitcast_fusion), channel_id=2, replica_groups=mesh['row'=4,'col'=8] {'row','col'}, dimensions={0}, use_global_device_ids=true | all-gather | bytes 287232 | tf_op jit(solution)/shard_map/all_gather | solution.py:31
  57.9 0.7 copy-done.4
  58.8 150.3 %all-gather.5.cloned.1.call-done = bf16[4096,4096]{1,0:T(8,128)(2,1)} async-done(((bf16[128,4096]{1,0:T(8,128)(2,1)}), bf16[4096,4096]{1,0:T(8,128)(2,1)}) %all-gather.5.cloned.1.call-update) | async-done | bytes 33554448 | tf_op jit(solution)/shard_map/all_gather | solution.py:60
  209.2 12.4 %convolution_convert_fusion = bf16[32,48,4096]{2,1,0:T(8,128)(2,1)S(1)} fusion(bf16[32,128,4096]{2,1,0:T(8,128)(2,1)} %bitcast.96, f32[32,128]{1,0:T(8,128)S(1)} %fusion.17, pred[32,128]{1,0:T(8,128)(4,1)S(1)} %compare_reduce_fusion.1), kind=kOutput, calls=%fused_computation | convolution fusion | flops 1617297408 | bytes 46157824 | tf_op jit(solution)/shard_map/dot_general | solution.py:61
  221.6 15.3 %fusion = f32[1536,768]{1,0:T(8,128)S(1)} fusion(bf16[1536,4096]{1,0:T(8,128)(2,1)S(1)} %bitcast.105, bf16[1,4096,768]{2,1,0:T(8,128)(2,1)} %param.10), kind=kOutput, calls=%fused_computation.1 | convolution fusion | flops 9663676416 | bytes 23592960 | tf_op jit(solution)/shard_map/dot_general | solution.py:77
  236.9 13.0 %multiply_convert_fusion = bf16[1536,768]{1,0:T(8,128)(2,1)S(1)} fusion(f32[1536,768]{1,0:T(8,128)S(1)} %fusion, bf16[1536,4096]{1,0:T(8,128)(2,1)S(1)} %bitcast.106, bf16[1,4096,768]{2,1,0:T(8,128)(2,1)} %param.9), kind=kOutput, calls=%fused_computation.5 | convolution fusion | flops 9670754304 | bytes 25952256 | tf_op jit(solution)/shard_map/dot_general | solution.py:76
  249.9 0.2 copy.45
  250.1 6.2 %convolution_convert_fusion.1 = bf16[1536,1024]{1,0:T(8,128)(2,1)} fusion(bf16[1536,768]{1,0:T(8,128)(2,1)S(1)} %bitcast.115, bf16[768,4096]{1,0:T(8,128)(2,1)} %bitcast.123), kind=kOutput, calls=%fused_computation.8 | convolution fusion | flops 2417491968 | bytes 7077888 | tf_op jit(solution)/shard_map/dot_general | solution.py:101
  256.3 3.8 all-to-all-start.3
  260.1 0.2 reduce-scatter.11.cloned.1.call-start
  260.9 0.2 copy-done.6
  261.1 1.0 fusion.10
  262.1 35.8 %all-to-all-done.3 = bf16[8,4,48,1024]{3,2,1,0:T(8,128)(2,1)S(1)} async-done(((bf16[8,4,48,1024]{3,2,1,0:T(8,128)(2,1)}), bf16[8,4,48,1024]{3,2,1,0:T(8,128)(2,1)S(1)}, u32[]{:S(2)}, u32[]{:S(2)}) %all-to-all-start.3) | async-done | bytes 3145760 | tf_op jit(solution)/shard_map/all_to_all | solution.py:102
  297.9 0.4 copy.55
  298.3 0.6 copy-done
  298.9 0.8 fusion.29
  299.6 2.2 convolution_add_fusion
  301.9 4.2 convolution_convert_fusion.2
  306.1 40.3 %all_to_all.20 = bf16[8,4,48,1024]{3,2,1,0:T(8,128)(2,1)S(1)} all-to-all(bf16[8,4,48,1024]{3,2,1,0:T(8,128)(2,1)S(1)} %bitcast.113), channel_id=1, replica_groups=mesh['row'=4,'col'=8] {'col'}, dimensions={0} | all-to-all | bytes 6291456 | tf_op jit(solution)/shard_map/all_to_all | solution.py:102
  346.4 0.5 copy.52
  346.9 0.5 copy-done.1
  347.4 0.8 fusion.28
  348.1 2.1 convolution_add_fusion.1
  350.3 4.2 convolution_convert_fusion.4
  354.5 40.3 %all_to_all.21 = bf16[8,4,48,1024]{3,2,1,0:T(8,128)(2,1)S(1)} all-to-all(bf16[8,4,48,1024]{3,2,1,0:T(8,128)(2,1)S(1)} %bitcast.114), channel_id=1, replica_groups=mesh['row'=4,'col'=8] {'col'}, dimensions={0} | all-to-all | bytes 6291456 | tf_op jit(solution)/shard_map/all_to_all | solution.py:102
  394.8 0.5 copy.46
  395.3 0.8 fusion.26
  396.1 2.1 convolution_add_fusion.3
  398.3 4.2 convolution_convert_fusion.3
  402.5 40.3 %all_to_all.22 = bf16[8,4,48,1024]{3,2,1,0:T(8,128)(2,1)S(1)} all-to-all(bf16[8,4,48,1024]{3,2,1,0:T(8,128)(2,1)S(1)} %bitcast.112), channel_id=1, replica_groups=mesh['row'=4,'col'=8] {'col'}, dimensions={0} | all-to-all | bytes 6291456 | tf_op jit(solution)/shard_map/all_to_all | solution.py:102
  442.8 0.5 copy.49
  443.3 0.8 fusion.27
  444.1 2.1 convolution_add_fusion.2
  446.2 1.0 slice_reduce_fusion
  447.1 0.9 convert_reduce_fusion
  448.0 0.6 fusion.23
  449.3 1.1 convert_bitcast_fusion
  450.5 1.1 convert_bitcast_fusion.1
  451.6 1.1 convert_bitcast_fusion.3
  452.6 34.6 %reduce-scatter.7.cloned.1.call-done = f32[1,128,1024]{2,1,0:T(8,128)} async-done(((f32[4,128,1024]{2,1,0:T(8,128)}), f32[1,128,1024]{2,1,0:T(8,128)}) %reduce-scatter.7.cloned.1.call-update) | async-done | bytes 524304 | tf_op jit(solution)/shard_map/reduce_scatter | solution.py:109
  487.2 1.1 convert_bitcast_fusion.2
  488.3 1.0 pad_maximum_fusion
  (38 shorter events, 1.0 us)
Async XLA Ops:
  7.2 202.0 %all-gather.5.cloned.1.call-start = ((), (), s32[]{:S(2)}) async-start(), calls=%async_computation.12 | async-start | bytes 34603008 | tf_op jit(solution)/shard_map/all_gather | solution.py:60
  57.9 0.7 copy-start.4
  250.1 6.2 %copy-start.2 = (bf16[4,8,48,768]{3,2,0,1:T(8,128)(2,1)}, bf16[4,8,48,768]{3,2,0,1:T(8,128)(2,1)S(1)}, u32[]{:S(2)}) copy-start(bf16[4,8,48,768]{3,2,0,1:T(8,128)(2,1)S(1)} %copy.45) | copy-start | bytes 7077892
  256.3 4.1 copy-start.5
  256.3 41.6 %all-to-all-start.3 = ((bf16[8,4,48,1024]{3,2,1,0:T(8,128)(2,1)}), bf16[8,4,48,1024]{3,2,1,0:T(8,128)(2,1)S(1)}, u32[]{:S(2)}, u32[]{:S(2)}) async-start(bf16[8,4,48,1024]{3,2,1,0:T(8,128)(2,1)} %bitcast.111), calls=%async_computation.6 | async-start | bytes 6291456 | tf_op jit(solution)/shard_map/all_to_all | solution.py:102
  260.1 189.2 %reduce-scatter.11.cloned.1.call-start = ((), (), s32[]{:S(2)}) async-start(), calls=%async_computation.11 | async-start | bytes 2621440 | tf_op jit(solution)/shard_map/reduce_scatter | solution.py:109
  260.4 0.6 copy-start.6
  297.9 1.0 copy-start
  299.6 2.2 copy-start.3
  301.8 148.6 %reduce-scatter.9.cloned.1.call-start = ((), (), s32[]{:S(2)}) async-start(), calls=%async_computation.10 | async-start | bytes 2621440 | tf_op jit(solution)/shard_map/reduce_scatter | solution.py:109
  346.4 1.0 copy-start.1
  350.3 101.3 %reduce-scatter.5.cloned.1.call-start = ((), (), s32[]{:S(2)}) async-start(), calls=%async_computation.8 | async-start | bytes 2621440 | tf_op jit(solution)/shard_map/reduce_scatter | solution.py:109
  398.2 89.0 %reduce-scatter.7.cloned.1.call-start = ((), (), s32[]{:S(2)}) async-start(), calls=%async_computation.9 | async-start | bytes 2621440 | tf_op jit(solution)/shard_map/reduce_scatter | solution.py:109
  444.1 3.1 copy-start.7
Sparse Core Ops, SparseCore 0:
  10.8 198.2 all-gather.4
  301.9 40.9 reduce-scatter.10
  350.4 40.8 reduce-scatter.8
  398.4 40.8 reduce-scatter.4
  446.3 40.8 reduce-scatter.6

commit v2 on v1

--- a/solution.py
+++ b/solution.py
@@ -1,12 +1,15 @@
 import jax
 import jax.numpy as jnp
 from jax import lax
+from jax.experimental import pallas as pl
+from jax.experimental.pallas import tpu as pltpu
 from jax.sharding import PartitionSpec as P
 
 BF16 = jnp.bfloat16
 F32 = jnp.float32
 AXES = ("row", "col")
-CHUNKS = 4
+CHUNK_EIGHTHS = (1, 2, 2, 2, 1)
+ROUTES_MIN = 1024 * 1024
 GATHER_LIMIT = 64 * 1024 * 1024
 
 
@@ -28,11 +31,119 @@
     prob_rows = -(-experts // tok)
     prob_sum = jnp.pad(jnp.sum(probs, axis=0), (0, prob_rows * tok - experts)).reshape(prob_rows, tok)
     packed = jnp.concatenate([expert_ids.astype(F32).T, weights.T, prob_sum], axis=0)
+    whole = lax.axis_size("row") * lax.axis_size("col") * tok * packed.dtype.itemsize
+    packed = jnp.pad(packed, ((0, max(0, -(-ROUTES_MIN // whole) - packed.shape[0])), (0, 0)))
     routes = lax.all_gather(packed, AXES, axis=0, tiled=False)
     ids = routes[:, :top_k].astype(jnp.int32)
     mix = routes[:, top_k : 2 * top_k]
-    prob_total = jnp.sum(routes[:, 2 * top_k :], axis=0).reshape(-1)[:experts]
+    prob_total = jnp.sum(routes[:, 2 * top_k : 2 * top_k + prob_rows], axis=0).reshape(-1)[:experts]
     return ids, mix, prob_total
+
+
+def flip(index, bit):
+    return index + bit - 2 * bit * ((index // bit) % 2)
+
+
+def gather_kernel(n_row, tok_ref, out_ref, own_sem, send_sems, recv_sems):
+    row, col = lax.axis_index("row"), lax.axis_index("col")
+    col_c, col_x, col_y = flip(col, 1), flip(col, 2), flip(col, 4)
+    col_d = flip(col_x, 4)
+
+    def peer_row(k):
+        there = row
+        bit = 1
+        while bit < n_row:
+            if k & bit:
+                there = flip(there, bit)
+            bit *= 2
+        return there
+
+    rows = [peer_row(k) for k in range(n_row)]
+
+    barrier = pltpu.get_barrier_semaphore()
+    peers = [(rows[k], col) for k in range(1, n_row)] + [(row, c) for c in (col_c, col_x, col_y)]
+    for peer in peers:
+        pl.semaphore_signal(barrier, inc=1, device_id=peer, device_id_type=pl.DeviceIdType.MESH)
+    pl.semaphore_wait(barrier, len(peers))
+
+    def copy(k, kind, src, dst, device):
+        return pltpu.make_async_remote_copy(
+            src_ref=src,
+            dst_ref=dst,
+            send_sem=send_sems.at[k, kind],
+            recv_sem=recv_sems.at[k, kind],
+            device_id=device,
+            device_id_type=pl.DeviceIdType.MESH,
+        )
+
+    started = []
+
+    def send(*args):
+        one = copy(*args)
+        one.start()
+        started.append(one)
+
+    def arrived(k, kind, ref):
+        copy(k, kind, ref, ref, (row, col_c)).wait_recv()
+
+    def spread(k):
+        origin = out_ref.at[rows[k], col]
+        source = tok_ref if k == 0 else origin
+        for half in range(2):
+            send(k, 1 + half, source.at[half], origin.at[half], (row, col_x))
+            send(k, 3 + half, source.at[half], origin.at[half], (row, col_y))
+        send(k, 7, source, origin, (row, col_c))
+
+    own = pltpu.make_async_copy(tok_ref, out_ref.at[row, col], own_sem)
+    for k in range(1, n_row):
+        send(k, 0, tok_ref, out_ref.at[row, col], (rows[k], col))
+    spread(0)
+    own.start()
+    for k in range(n_row):
+        if k + 1 < n_row:
+            arrived(k + 1, 0, out_ref.at[rows[k + 1], col])
+            spread(k + 1)
+        from_x, from_y = out_ref.at[rows[k], col_x], out_ref.at[rows[k], col_y]
+        arrived(k, 3, from_y.at[0])
+        send(k, 5, from_y.at[0], from_y.at[0], (row, col_x))
+        arrived(k, 2, from_x.at[1])
+        send(k, 6, from_x.at[1], from_x.at[1], (row, col_y))
+        arrived(k, 1, from_x.at[0])
+        send(k, 8, from_x, from_x, (row, col_c))
+        arrived(k, 4, from_y.at[1])
+        send(k, 9, from_y, from_y, (row, col_c))
+    for k in range(n_row):
+        diagonal = out_ref.at[rows[k], col_d]
+        arrived(k, 5, diagonal.at[0])
+        arrived(k, 6, diagonal.at[1])
+        send(k, 10, diagonal, diagonal, (row, col_c))
+    for k in range(n_row):
+        for kind, place in ((7, col), (8, col_x), (9, col_y), (10, col_d)):
+            arrived(k, kind, out_ref.at[rows[k], flip(place, 1)])
+    own.wait()
+    for one in started:
+        one.wait_send()
+
+
+def gather_tokens(tokens, n_row, n_col):
+    tok, width = tokens.shape
+    if n_col != 8 or n_row & (n_row - 1):
+        return lax.all_gather(tokens, AXES, axis=0, tiled=False)
+    kinds = 11
+    out = pl.pallas_call(
+        lambda *refs: gather_kernel(n_row, *refs),
+        out_shape=jax.ShapeDtypeStruct((n_row, n_col, 2, tok // 2, width), tokens.dtype),
+        in_specs=[pl.BlockSpec(memory_space=pltpu.VMEM)],
+        out_specs=pl.BlockSpec(memory_space=pl.ANY),
+        scratch_shapes=[
+            pltpu.SemaphoreType.DMA(()),
+            pltpu.SemaphoreType.DMA((n_row, kinds)),
+            pltpu.SemaphoreType.DMA((n_row, kinds)),
+        ],
+        compiler_params=pltpu.CompilerParams(collective_id=0, has_side_effects=True),
+        cost_estimate=pl.CostEstimate(flops=0, bytes_accessed=300 * 1024 * 1024, transcendentals=0),
+    )(tokens.reshape(2, tok // 2, width))
+    return out.reshape(n_row * n_col, tok, width)
 
 
 def local(tokens, router_logits, expert_ids, w_gate, w_up, w_down):
@@ -57,7 +168,7 @@
         hit = jnp.any(ids == me, axis=1)
         slot = slots_before(hit)
         pick = (hit[:, None, :] & (slot[:, None, :] == places[None, :, None])).astype(BF16)
-        everyone = lax.all_gather(tokens, AXES, axis=0, tiled=False)
+        everyone = gather_tokens(tokens, n_row, n_col)
         rows = lax.dot_general(
             pick, everyone, (((2,), (1,)), ((0,), (0,))), preferred_element_type=F32
         ).astype(BF16)
@@ -94,10 +205,12 @@
 
     high, low = table(high), table(low)
 
-    step = width // CHUNKS
     parts = []
-    for chunk in range(CHUNKS):
-        down = w_down[0][:, chunk * step : (chunk + 1) * step]
+    start = 0
+    for eighths in CHUNK_EIGHTHS:
+        step = eighths * width // 8
+        down = w_down[0][:, start : start + step]
+        start += step
         result = jnp.dot(hidden, down, preferred_element_type=F32).astype(BF16)
         back = lax.all_to_all(
             result.reshape(n_col, n_row, capacity, step), "col", split_axis=0, concat_axis=0, tiled=True

time: 498 us -> 480 us (0.964)
  Pallas kernels: 0 us -> 174 us
  waiting for transfers between devices: 222 us -> 81.5 us
  blocking collectives: 167 us -> 104 us
    pallas_call x0 -> x1, Pallas kernels: none -> 174 us  [gather_tokens(): pl.pallas_call(lambda *refs: gather_kernel(n_row, *refs), out_shape=jax.S...]
    all_gather x1, waiting for transfers between devices: 150 us -> 0.02 us  [exchange_routes(): routes = lax.all_gather(packed, AXES, axis=0, tiled=False)]
    all_gather x1 -> x0, blocking collectives: 46.2 us -> none  [exchange_routes(): routes = lax.all_gather(packed, AXES, axis=0, tiled=False)]
    all_to_all x3, blocking collectives: 121 us -> 104 us  [local(): lax.all_to_all(result.reshape(n_col, n_row, capacity, step), 'col', split...]
    all_to_all x1 -> x2, waiting for transfers between devices: 35.8 us -> 48.3 us  [local(): lax.all_to_all(result.reshape(n_col, n_row, capacity, step), 'col', split...]
    dot_general x4 -> x5, matrix products: 18.9 us -> 21.6 us  [local(): result = jnp.dot(hidden, down, preferred_element_type=F32).astype(BF16)]
    reduce_scatter x4 -> x5, waiting for transfers between devices: 34.6 us -> 33.1 us  [local(): total = lax.psum_scatter(partial, 'row', scatter_dimension=0, tiled=True)]
  transfers between devices with their start and end apart: 6 -> 8, of which waited for: 3 -> 4; matrix products, arithmetic and copies ran while one was open for 7% -> 9% of each run, Pallas kernels for 0% -> 36%
where the time goes in v2:
time: 480 us; the launch traced here: 479 us
  Pallas kernels  174 us (36%)
  blocking collectives  104 us (22%)
  waiting for transfers between devices  81.5 us (17%)
  matrix products  75.3 us (16%)
  between operations  16.2 us (3%)
  other arithmetic  14.3 us (3%)
  starting transfers between devices  8.67 us (2%)
  local copies, waits for them, and re-layouts  4.85 us (1%)
    pallas_call x1, Pallas kernels, gather_tokens(): pl.pallas_call(lambda *refs: gather_kernel(n_row, *refs), out_shape=jax.S...  174 us
    all_to_all x3, blocking collectives, local(): lax.all_to_all(result.reshape(n_col, n_row, capacity, step), 'col', split...  104 us
    all_to_all x2, waiting for transfers between devices, local(): lax.all_to_all(result.reshape(n_col, n_row, capacity, step), 'col', split...  48.3 us
    reduce_scatter x5, waiting for transfers between devices, local(): total = lax.psum_scatter(partial, 'row', scatter_dimension=0, tiled=True)  33.1 us
    dot_general x5, matrix products, local(): result = jnp.dot(hidden, down, preferred_element_type=F32).astype(BF16)  21.6 us
    dot_general x1, matrix products, local(): up_act = jnp.dot(shaped, w_up[0], preferred_element_type=F32)  15.3 us
    dot_general x1, matrix products, local(): gate_act = jnp.dot(shaped, w_gate[0], preferred_element_type=F32)  13 us
    dot_general x1, matrix products, local(): lax.dot_general(pick, everyone, (((2,), (1,)), ((0,), (0,))), preferred_e...  12.4 us
  transfers between devices with their start and end apart: 8, of which 4 were waited for; matrix products, arithmetic and copies ran while one was open for 9% of the time, Pallas kernels for 36%

profile of v2, /device:TPU:0, one launch (start us, length us, event | category | flops | bytes accessed | tf_op | source)
XLA Modules:
  0.0 478.8 jit_solution(14142528142035789416)
XLA Ops:
  7.2 0.7 reduce_max.9
  7.9 0.7 fusion.23
  8.7 0.7 convert_bitcast_fusion
  9.4 0.8 fusion.25
  10.2 0.7 select_reduce_fusion
  11.0 0.6 select_maximum_fusion
  11.6 174.1 %shard_map.77 = bf16[4,8,2,64,4096]{4,3,2,1,0:T(8,128)(2,1)} custom-call(bf16[2,64,4096]{2,1,0:T(8,128)(2,1)} %bitcast.134), custom_call_target="tpu_custom_call" | custom-call | bytes 314572800 | tf_op jit(solution)/shard_map/pallas_call | solution.py:133
  185.8 1.0 compare_reduce_fusion.1
  186.9 12.4 %convolution_convert_fusion = bf16[32,48,4096]{2,1,0:T(8,128)(2,1)S(1)} fusion(bf16[32,128,4096]{2,1,0:T(8,128)(2,1)} %bitcast.106, f32[32,128]{1,0:T(8,128)S(1)} %fusion.18, pred[32,128]{1,0:T(8,128)(4,1)S(1)} %compare_reduce_fusion.1), kind=kOutput, calls=%fused_computation | convolution fusion | flops 1617297408 | bytes 46157824 | tf_op jit(solution)/shard_map/dot_general | solution.py:172
  199.3 15.3 %fusion = f32[1536,768]{1,0:T(8,128)S(1)} fusion(bf16[1536,4096]{1,0:T(8,128)(2,1)S(1)} %bitcast.113, bf16[1,4096,768]{2,1,0:T(8,128)(2,1)} %param.10), kind=kOutput, calls=%fused_computation.1 | convolution fusion | flops 9663676416 | bytes 23592960 | tf_op jit(solution)/shard_map/dot_general | solution.py:188
  214.6 13.0 %multiply_convert_fusion = bf16[1536,768]{1,0:T(8,128)(2,1)S(1)} fusion(f32[1536,768]{1,0:T(8,128)S(1)} %fusion, bf16[1536,4096]{1,0:T(8,128)(2,1)S(1)} %bitcast.114, bf16[1,4096,768]{2,1,0:T(8,128)(2,1)} %param.9), kind=kOutput, calls=%fused_computation.5 | convolution fusion | flops 9670754304 | bytes 25952256 | tf_op jit(solution)/shard_map/dot_general | solution.py:187
  227.8 4.3 convolution_convert_fusion.5
  232.0 3.8 all-to-all-start
  235.9 1.0 slice_convert_fusion
  236.9 6.4 %convolution_convert_fusion.3 = bf16[1536,1024]{1,0:T(8,128)(2,1)} fusion(bf16[1536,768]{1,0:T(8,128)(2,1)} %bitcast.127, bf16[768,4096]{1,0:T(8,128)(2,1)} %bitcast.142), kind=kOutput, calls=%fused_computation.10 | convolution fusion | flops 2417491968 | bytes 7077888 | tf_op jit(solution)/shard_map/dot_general | solution.py:214
  243.3 13.3 %all-to-all-done = bf16[8,4,48,512]{3,2,1,0:T(8,128)(2,1)S(1)} async-done(((bf16[8,4,48,512]{3,2,1,0:T(8,128)(2,1)}), bf16[8,4,48,512]{3,2,1,0:T(8,128)(2,1)S(1)}, u32[]{:S(2)}, u32[]{:S(2)}) %all-to-all-start) | async-done | bytes 1572896 | tf_op jit(solution)/shard_map/all_to_all | solution.py:215
  256.6 4.4 all-to-all-start.1
  261.8 0.5 fusion.27
  262.3 1.5 convolution_add_fusion.4
  263.9 35.0 %all-to-all-done.1 = bf16[8,4,48,1024]{3,2,1,0:T(8,128)(2,1)} async-done(((bf16[8,4,48,1024]{3,2,1,0:T(8,128)(2,1)}), bf16[8,4,48,1024]{3,2,1,0:T(8,128)(2,1)}, u32[]{:S(2)}, u32[]{:S(2)}) %all-to-all-start.1) | async-done | bytes 3145760 | tf_op jit(solution)/shard_map/all_to_all | solution.py:215
  298.9 2.4 copy.38
  301.3 0.8 fusion.28
  302.0 2.2 convolution_add_fusion.2
  304.3 4.2 convolution_convert_fusion.2
  308.5 40.3 %all_to_all.25 = bf16[8,4,48,1024]{3,2,1,0:T(8,128)(2,1)S(1)} all-to-all(bf16[8,4,48,1024]{3,2,1,0:T(8,128)(2,1)S(1)} %bitcast.124), channel_id=1, replica_groups=mesh['row'=4,'col'=8] {'col'}, dimensions={0} | all-to-all | bytes 6291456 | tf_op jit(solution)/shard_map/all_to_all | solution.py:215
  348.8 0.5 copy.41
  349.3 0.8 fusion.29
  350.0 2.1 convolution_add_fusion.1
  352.2 4.2 convolution_convert_fusion.1
  356.4 40.3 %all_to_all.26 = bf16[8,4,48,1024]{3,2,1,0:T(8,128)(2,1)S(1)} all-to-all(bf16[8,4,48,1024]{3,2,1,0:T(8,128)(2,1)S(1)} %bitcast.125), channel_id=1, replica_groups=mesh['row'=4,'col'=8] {'col'}, dimensions={0} | all-to-all | bytes 6291456 | tf_op jit(solution)/shard_map/all_to_all | solution.py:215
  396.7 0.5 copy.44
  397.2 0.8 fusion.30
  398.0 2.1 convolution_add_fusion
  400.4 2.5 convolution_convert_fusion.4
  402.9 23.4 %all_to_all.27 = bf16[8,4,48,512]{3,2,1,0:T(8,128)(2,1)S(1)} all-to-all(bf16[8,4,48,512]{3,2,1,0:T(8,128)(2,1)S(1)} %bitcast.133), channel_id=1, replica_groups=mesh['row'=4,'col'=8] {'col'}, dimensions={0} | all-to-all | bytes 3145728 | tf_op jit(solution)/shard_map/all_to_all | solution.py:215
  426.4 0.5 fusion.31
  427.0 1.5 convolution_add_fusion.3
  428.5 1.0 slice_reduce_fusion
  429.5 0.9 convert_reduce_fusion
  430.3 0.6 fusion.24
  431.6 1.0 bitcast_dynamic-update-slice_fusion.4
  432.6 1.1 bitcast_dynamic-update-slice_fusion.2
  433.7 1.1 bitcast_dynamic-update-slice_fusion.1
  434.8 5.4 %reduce-scatter.12.cloned.1.call-done = f32[1,128,1024]{2,1,0:T(8,128)} async-done(((f32[4,128,1024]{2,1,0:T(8,128)}), f32[1,128,1024]{2,1,0:T(8,128)}) %reduce-scatter.12.cloned.1.call-update) | async-done | bytes 524304 | tf_op jit(solution)/shard_map/reduce_scatter | solution.py:222
  440.2 1.1 bitcast_dynamic-update-slice_fusion
  441.3 27.6 %reduce-scatter.14.cloned.1.call-done = f32[1,128,512]{2,1,0:T(8,128)} async-done(((f32[4,128,512]{2,1,0:T(8,128)}), f32[1,128,512]{2,1,0:T(8,128)}) %reduce-scatter.14.cloned.1.call-update) | async-done | bytes 262160 | tf_op jit(solution)/shard_map/reduce_scatter | solution.py:222
  468.9 1.0 bitcast_dynamic-update-slice_fusion.3
  469.9 1.0 copy-done.2
  (37 shorter events, 1.9 us)
Async XLA Ops:
  7.2 178.6 %all-gather.3.cloned.1.call-start = ((), (), s32[]{:S(2)}) async-start(), calls=%async_computation.15 | async-start | bytes 1081344 | tf_op jit(solution)/shard_map/all_gather | solution.py:36
  227.8 4.3 copy-start
  232.0 24.5 %all-to-all-start = ((bf16[8,4,48,512]{3,2,1,0:T(8,128)(2,1)}), bf16[8,4,48,512]{3,2,1,0:T(8,128)(2,1)S(1)}, u32[]{:S(2)}, u32[]{:S(2)}) async-start(bf16[8,4,48,512]{3,2,1,0:T(8,128)(2,1)} %bitcast.132), calls=%async_computation | async-start | bytes 3145728 | tf_op jit(solution)/shard_map/all_to_all | solution.py:215
  256.6 42.3 %all-to-all-start.1 = ((bf16[8,4,48,1024]{3,2,1,0:T(8,128)(2,1)}), bf16[8,4,48,1024]{3,2,1,0:T(8,128)(2,1)}, u32[]{:S(2)}, u32[]{:S(2)}) async-start(bf16[8,4,48,1024]{3,2,1,0:T(8,128)(2,1)} %bitcast.123), calls=%async_computation.2 | async-start | bytes 6291456 | tf_op jit(solution)/shard_map/all_to_all | solution.py:215
  261.0 170.6 %reduce-scatter.6.cloned.1.call-start = ((), (), s32[]{:S(2)}) async-start(), calls=%async_computation.10 | async-start | bytes 1310720 | tf_op jit(solution)/shard_map/reduce_scatter | solution.py:222
  263.8 168.8 %reduce-scatter.8.cloned.1.call-start = ((), (), s32[]{:S(2)}) async-start(), calls=%async_computation.11 | async-start | bytes 2621440 | tf_op jit(solution)/shard_map/reduce_scatter | solution.py:222
  302.0 2.2 copy-start.1
  304.2 129.5 %reduce-scatter.10.cloned.1.call-start = ((), (), s32[]{:S(2)}) async-start(), calls=%async_computation.12 | async-start | bytes 2621440 | tf_op jit(solution)/shard_map/reduce_scatter | solution.py:222
  352.2 88.1 %reduce-scatter.12.cloned.1.call-start = ((), (), s32[]{:S(2)}) async-start(), calls=%async_computation.13 | async-start | bytes 2621440 | tf_op jit(solution)/shard_map/reduce_scatter | solution.py:222
  400.1 68.8 %reduce-scatter.14.cloned.1.call-start = ((), (), s32[]{:S(2)}) async-start(), calls=%async_computation.14 | async-start | bytes 1310720 | tf_op jit(solution)/shard_map/reduce_scatter | solution.py:222
  469.9 1.0 copy-start.2
Sparse Core Ops, SparseCore 0:
  11.7 113.4 all-gather.2
  264.7 25.8 reduce-scatter.5
  304.3 39.9 reduce-scatter.7
  352.3 39.9 reduce-scatter.9
  400.2 39.9 reduce-scatter.11
  442.4 26.4 reduce-scatter.13
